TPU v7x, 256 devices: a whole 4x4x8 slice. The times are simulated.
256 devices in a mesh: dp: 32 (over z, y_hi, core), mp: 8 (over x, y_lo).
Axes of the slice: x: 4, y: 4 (y_hi: 2, y_lo: 2; y = y_hi * 2 + y_lo), z: 8, core: 2. Of those that a mesh axis runs over, the one named last changes fastest.
Arguments:
- activations: bfloat16 [16384, 28672], P('dp', 'mp'), may hold values from -200 to 200
- weight: bfloat16 [8192, 28672], P(None, ('mp', 'dp')), may hold values from -25 to 25
- thresholds: float32 [8192], P('dp'), may hold values from 0.5 to 1.5
Outputs:
- pruned: bfloat16 [8192, 28672], P('dp', 'mp')
All inputs are finite; a program needn't handle non-finite values.
Results may differ from a plain program's by a relative error of at most 0.0004.
Values may be sent and summed in bfloat16 or wider, within the bound.
A program may use at most 64 MiB of HBM per device.

v0:
```python
import jax
import jax.numpy as jnp
from jax import lax
from jax.sharding import PartitionSpec as P

IN = 28672


gate_slope = 2.0
small_eps = 1e-06


def sent_to_all(shard, axis):
    copies = jnp.broadcast_to(shard, (lax.axis_size(axis), *shard.shape))
    return lax.all_to_all(copies, axis, split_axis=0, concat_axis=0, tiled=True)


def over_copies(shard, axis):
    return sent_to_all(shard, axis).sum(axis=0)


def soft_prune(block, col_norm, row_total, limit):
    wide = block.astype(jnp.float32)
    scores = jnp.abs(wide) * col_norm[None, :]
    row_mean = row_total[:, None] / IN + small_eps
    kept_share = jnp.clip((scores / row_mean - limit[:, None]) * gate_slope + 0.5, 0.0, 1.0)
    return (wide * kept_share).astype(jnp.bfloat16)


def per_device(activations, weight, thresholds):
    partial_value = jnp.sum(jnp.square(activations.astype(jnp.float32)), axis=0)
    relaid = lax.all_to_all(weight, "dp", split_axis=0, concat_axis=1, tiled=True)
    squares = over_copies(partial_value, "dp")
    col_norm = jnp.sqrt(squares)
    row_part = jnp.sum(jnp.abs(relaid.astype(jnp.float32)) * col_norm[None, :], axis=1)
    row_total = over_copies(row_part, "mp")
    return soft_prune(relaid, col_norm, row_total, thresholds)


def solution(mesh):
    placed = (P("dp", "mp"), P(None, ("mp", "dp")), P("dp"))
    return jax.shard_map(
        per_device, mesh=mesh, in_specs=placed, out_specs=P("dp", "mp"), check_vma=False
    )
```

profile of v0, /device:TPU:1, one launch (start us, length us, event | category | flops | bytes accessed | tf_op | source)
XLA Modules:
  0.0 98.6 jit_solution(1914880998920261515)
XLA Ops:
  0.0 0.0 copy-start
  0.0 2.9 %multiply_reduce_fusion = f32[3584]{0:T(1024)S(1)} fusion(bf16[512,3584]{1,0:T(8,128)(2,1)} %param.3), kind=kLoop, calls=%fused_computation | loop fusion | flops 5501440 | bytes 3684352 | tf_op jit(solution)/shard_map/reduce_sum | solution.py:31
  2.9 1.0 %broadcast_in_dim.4 = f32[32,1,3584]{2,1,0:T(1,128)} broadcast(f32[3584]{0:T(1024)S(1)} %multiply_reduce_fusion), dimensions={2} | broadcast | bytes 473088 | tf_op jit(solution)/shard_map/broadcast_in_dim | solution.py:14
  3.9 12.7 %all-to-all-start.1 = ((f32[32,1,3584]{2,1,0:T(1,128)}), f32[32,1,3584]{2,1,0:T(1,128)S(1)}, u32[]{:S(2)}, u32[]{:S(2)}) async-start(f32[32,1,3584]{2,1,0:T(1,128)} %broadcast_in_dim.4), calls=%async_computation.1 | async-start | bytes 917504 | tf_op jit(solution)/shard_map/all_to_all | solution.py:15
  16.7 0.0 copy-done
  16.7 1.4 %copy.23 = bf16[14,32,8,256]{3,2,0,1:T(8,128)(2,1)} copy(bf16[14,32,8,256]{3,2,1,0:T(8,128)(2,1)S(1)} %bitcast.26) | data formatting | bytes 3670016 | tf_op jit(solution)/shard_map/all_to_all | solution.py:32
  18.0 0.0 copy-start.1
  18.0 14.1 %all-to-all-done.1 = f32[32,1,3584]{2,1,0:T(1,128)S(1)} async-done(((f32[32,1,3584]{2,1,0:T(1,128)}), f32[32,1,3584]{2,1,0:T(1,128)S(1)}, u32[]{:S(2)}, u32[]{:S(2)}) %all-to-all-start.1) | async-done | bytes 458784 | tf_op jit(solution)/shard_map/all_to_all | solution.py:15
  32.2 5.8 %all-to-all-start = ((bf16[32,256,112]{1,2,0:T(8,128)(2,1)}), bf16[32,256,112]{1,2,0:T(8,128)(2,1)S(1)}, u32[]{:S(2)}, u32[]{:S(2)}) async-start(bf16[32,256,112]{1,2,0:T(8,128)(2,1)} %bitcast.25), calls=%async_computation | async-start | bytes 3670016 | tf_op jit(solution)/shard_map/all_to_all | solution.py:32
  38.0 0.3 reduce_sum.37
  38.2 0.1 sqrt.12
  38.3 44.2 %all-to-all-done = bf16[32,256,112]{1,2,0:T(8,128)(2,1)S(1)} async-done(((bf16[32,256,112]{1,2,0:T(8,128)(2,1)}), bf16[32,256,112]{1,2,0:T(8,128)(2,1)S(1)}, u32[]{:S(2)}, u32[]{:S(2)}) %all-to-all-start) | async-done | bytes 1835040 | tf_op jit(solution)/shard_map/all_to_all | solution.py:32
  82.6 0.6 fusion.1
  83.1 9.0 %all_to_all.25 = f32[8,1,256]{2,1,0:T(1,128)S(1)} all-to-all(f32[8,1,256]{2,1,0:T(1,128)S(1)} %broadcast_in_dim.5), channel_id=1, replica_groups=mesh['dp'=32,'mp'=8] {'mp'}, dimensions={0} | all-to-all | bytes 16384 | tf_op jit(solution)/shard_map/all_to_all | solution.py:15
  92.1 0.0 copy-done.1
  92.1 2.6 %fusion.8 = bf16[256,3584]{0,1:T(8,128)(2,1)} fusion(bf16[32,256,112]{1,2,0:T(8,128)(2,1)S(1)} %all-to-all-done, f32[256]{0:T(256)S(1)} %copy-done.1, f32[256]{0:T(256)S(1)} %multiply_add_fusion, f32[3584]{0:T(1024)S(1)} %sqrt.11), kind=kLoop, calls=%fused_computation.12 | loop fusion | flops 9175040 | bytes 3686400 | tf_op jit(solution)/shard_map/convert_element_type | solution.py:27
  94.8 3.8 %copy.18 = bf16[256,3584]{1,0:T(8,128)(2,1)} copy(bf16[256,3584]{0,1:T(8,128)(2,1)} %fusion.8) | data formatting | bytes 3670016 | tf_op jit(solution)/shard_map/convert_element_type | solution.py:27
  (4 shorter events, 0.1 us)
Async XLA Ops:
  0.0 16.7 %copy-start = (bf16[8192,112]{0,1:T(8,128)(2,1)S(1)}, bf16[8192,112]{0,1:T(8,128)(2,1)}, u32[]{:S(2)}) copy-start(bf16[8192,112]{0,1:T(8,128)(2,1)} %param.4) | copy-start | bytes 5505028
  3.9 28.2 %all-to-all-start.1 = ((f32[32,1,3584]{2,1,0:T(1,128)}), f32[32,1,3584]{2,1,0:T(1,128)S(1)}, u32[]{:S(2)}, u32[]{:S(2)}) async-start(f32[32,1,3584]{2,1,0:T(1,128)} %broadcast_in_dim.4), calls=%async_computation.1 | async-start | bytes 917504 | tf_op jit(solution)/shard_map/all_to_all | solution.py:15
  18.0 74.1 %copy-start.1 = (f32[256]{0:T(256)S(1)}, f32[256]{0:T(256)}, u32[]{:S(2)}) copy-start(f32[256]{0:T(256)} %param.5) | copy-start | bytes 3076
  32.2 50.4 %all-to-all-start = ((bf16[32,256,112]{1,2,0:T(8,128)(2,1)}), bf16[32,256,112]{1,2,0:T(8,128)(2,1)S(1)}, u32[]{:S(2)}, u32[]{:S(2)}) async-start(bf16[32,256,112]{1,2,0:T(8,128)(2,1)} %bitcast.25), calls=%async_computation | async-start | bytes 3670016 | tf_op jit(solution)/shard_map/all_to_all | solution.py:32
where the time goes:
time: 99.9 us; the launch traced here: 98.6 us
  waiting for transfers between devices  58.4 us (58%)
  starting transfers between devices  18.5 us (19%)
  blocking collectives  8.96 us (9%)
  other arithmetic  6.43 us (6%)
  local copies, waits for them, and re-layouts  6.26 us (6%)
    all_to_all x1, waiting for transfers between devices, per_device(): lax.all_to_all(weight, 'dp', split_axis=0, concat_axis=1, tiled=True)  44.2 us
    all_to_all x1, waiting for transfers between devices, sent_to_all(): return lax.all_to_all(copies, axis, split_axis=0, concat_axis=0, tiled=True)  14.1 us
    all_to_all x1, starting transfers between devices, sent_to_all(): return lax.all_to_all(copies, axis, split_axis=0, concat_axis=0, tiled=True)  12.7 us
    all_to_all x1, blocking collectives, sent_to_all(): return lax.all_to_all(copies, axis, split_axis=0, concat_axis=0, tiled=True)  8.96 us
    all_to_all x1, starting transfers between devices, per_device(): lax.all_to_all(weight, 'dp', split_axis=0, concat_axis=1, tiled=True)  5.78 us
    convert_element_type x1, local copies, waits for them, and re-layouts, soft_prune(): return (wide * kept_share).astype(jnp.bfloat16)  3.8 us
    reduce_sum x1, other arithmetic, per_device(): partial_value = jnp.sum(jnp.square(activations.astype(jnp.float32)), axis=0)  2.92 us
    convert_element_type x1, other arithmetic, soft_prune(): return (wide * kept_share).astype(jnp.bfloat16)  2.65 us
  transfers between devices with their start and end apart: 2, of which 2 were waited for; matrix products, arithmetic and copies ran while one was open for 2% of the time, Pallas kernels for 0%

commit v1 on v0

v1 whole, which is shorter than its diff:
```python
import functools

import jax
import jax.numpy as jnp
from jax import lax
from jax.experimental import pallas as pl
from jax.experimental.pallas import tpu as pltpu
from jax.sharding import PartitionSpec as P

IN = 28672
LANES = 128
MESH = pl.DeviceIdType.MESH

gate_slope = 2.0
small_eps = 1e-06


FIRST = 9
SECOND = 20


def kernel(
    n_dp, n_mp, act_hbm, wt_hbm, thr_hbm, out_ref,
    act, wt, got, sq_send, sq_got, row_send, row_got, tot_send, tot_got, norms, limits, scale_a, scale_b,
    act_sem, local_sem, bulk_send, bulk_recv, small_send, small_recv,
):
    d, m = lax.axis_index("dp"), lax.axis_index("mp")
    cols, outs = wt_hbm.shape
    rows = outs // n_dp
    groups = n_dp // 8
    per_group = cols * 8 // LANES
    chunks = groups * per_group
    steps = act_sem.shape[0]
    tokens = act_hbm.shape[0] // steps
    depth = n_dp // 4
    peers = n_dp - 1

    z, high, core = lax.div(d, 4), lax.rem(lax.div(d, 2), 2), lax.rem(d, 2)
    sides = ((1 - high) * 2 + core, (1 - high) * 2 + 1 - core, high * 2 + 1 - core, high * 2 + core)
    hops = [depth // 2 + (k // 2 if k % 2 == 0 else -((k + 1) // 2)) for k in range(depth)]
    partners = [(side, hop) for side in range(4) for hop in hops][:-1]

    def target(i):
        side, hop = partners[i]
        return lax.rem(z + hop, depth) * 4 + sides[side]

    def mp_peer(i):
        return lax.rem(m + i, n_mp)

    def act_copy(i):
        span = pl.ds(pl.multiple_of(i * tokens, tokens), tokens)
        return pltpu.make_async_copy(act_hbm.at[span], act.at[span], act_sem.at[i])

    def block(i):
        return pl.ds(pl.multiple_of(i * rows, rows), rows)

    def place_of(i, n=1):
        return pl.ds(pl.multiple_of(i * cols, 16), n * cols)

    def landed(i):
        return bulk_recv.at[min(i // depth, 3) + max(i - 3 * depth, 0)]

    def bulk_copy(i):
        to = target(i)
        return pltpu.make_async_remote_copy(
            src_ref=wt_hbm.at[:, block(to)], dst_ref=got.at[place_of(d)],
            send_sem=bulk_send, recv_sem=landed(i), device_id=(to, m), device_id_type=MESH,
        )

    def small_copy(src, dst, n, i):
        to = target(i)
        return pltpu.make_async_remote_copy(
            src_ref=src.at[to], dst_ref=dst.at[d], send_sem=small_send.at[n], recv_sem=small_recv.at[n],
            device_id=(to, m), device_id_type=MESH,
        )

    def tot_copy(i):
        return pltpu.make_async_remote_copy(
            src_ref=tot_send, dst_ref=tot_got.at[m], send_sem=small_send.at[2], recv_sem=small_recv.at[2],
            device_id=(d, mp_peer(i)), device_id_type=MESH,
        )

    def wait_for(ref, sem):
        pltpu.make_async_copy(ref, ref, sem).wait()

    def loop(lo, hi, body):
        lax.fori_loop(lo, hi, lambda i, c: (body(i), c)[1], 0)

    with jax.named_scope("local"):
        loop(0, steps, lambda i: act_copy(i).start())
        wt_local = pltpu.make_async_copy(wt_hbm, wt, local_sem.at[0])
        wt_local.start()
        own = pltpu.make_async_copy(wt_hbm.at[:, block(d)], got.at[place_of(d)], local_sem.at[1])
        own.start()
        limit_local = pltpu.make_async_copy(thr_hbm, limits, local_sem.at[2])
        limit_local.start()

    with jax.named_scope("signal"):
        barrier = pltpu.get_barrier_semaphore()
        for i in range(peers):
            pl.semaphore_signal(barrier, inc=1, device_id=(target(i), m), device_id_type=MESH)
        for i in range(1, n_mp):
            pl.semaphore_signal(barrier, inc=1, device_id=(d, mp_peer(i)), device_id_type=MESH)

    with jax.named_scope("squares"):
        def add_squares(i, sums):
            act_copy(i).wait()
            base = pl.multiple_of(i * tokens, tokens)
            out = []
            for j in range(chunks):
                x = act[pl.ds(base, tokens), j * LANES:(j + 1) * LANES].astype(jnp.float32)
                out.append(sums[j] + jnp.sum((x * x).reshape(tokens // 8, 8, LANES), axis=0))
            return tuple(out)

        sums = lax.fori_loop(0, steps, add_squares, tuple(jnp.zeros((8, LANES), jnp.float32) for _ in range(chunks)))
        sums = [jnp.sum(s, axis=0, keepdims=True) for s in sums]
        lane = lax.broadcasted_iota(jnp.int32, (1, LANES), 1)
        for q in range(groups):
            for u in range(8):
                shift = (LANES - cols) * u
                first = sums[per_group * q + max(u - 1, 0)]
                second = sums[per_group * q + min(u, per_group - 1)]
                if u:
                    first = pltpu.roll(first, shift, 1)
                    second = pltpu.roll(second, shift, 1)
                row = jnp.where(lane < shift, first, second)
                sq_send[8 * q + u] = jnp.where(lane < cols, row, 0.0)

    with jax.named_scope("barrier"):
        pl.semaphore_wait(barrier, peers + n_mp - 1)

    with jax.named_scope("issue"):
        for i in range(peers):
            small_copy(sq_send, sq_got, 0, i).start()
        for i in range(FIRST):
            bulk_copy(i).start()
        sq_got[d] = sq_send[d]
        wt_local.wait()

    with jax.named_scope("wait_sq"):
        wait_for(sq_got.at[:peers], small_recv.at[0])

    with jax.named_scope("rowpart"):
        squares = jnp.sum(sq_got[...].reshape(n_dp // 8, 8, LANES), axis=0)
        squares = jnp.sum(squares, axis=0, keepdims=True)
        norm = jnp.broadcast_to(jnp.sqrt(squares), (LANES, LANES)).T[:cols]

        def row_part(r):
            for h in range(rows // LANES):
                w = wt[:, pl.ds(pl.multiple_of(r * rows + h * LANES, LANES), LANES)].astype(jnp.float32)
                part = jnp.sum((jnp.abs(w) * norm).reshape(cols // 8, 8, LANES), axis=0)
                row_send[r, :, h * LANES:(h + 1) * LANES] = jnp.sum(part, axis=0, keepdims=True)
            row_send[r, :, rows:] = squares

        loop(0, n_dp, row_part)
    with jax.named_scope("send_row"):
        for i in range(peers):
            small_copy(row_send, row_got, 1, i).start()
        for i in range(FIRST, SECOND):
            bulk_copy(i).start()
        row_got[d] = row_send[d]
    with jax.named_scope("wait_row"):
        wait_for(row_got.at[:peers], small_recv.at[1])

    with jax.named_scope("tot"):
        tot_send[...] = jnp.sum(row_got[:, :, :rows], axis=0)
        for i in range(1, n_mp):
            tot_copy(i).start()
        for i in range(SECOND, peers):
            bulk_copy(i).start()
        tot_got[m] = tot_send[...]
    with jax.named_scope("norms"):
        for q in range(groups):
            for t in range(per_group):
                shift = (LANES - cols) * t
                first = row_got[8 * q + t, :, rows:]
                second = row_got[8 * q + t + 1, :, rows:]
                first = pltpu.roll(first, LANES - shift, 1) if shift else first
                second = pltpu.roll(second, cols - shift, 1)
                norms[per_group * q + t] = jnp.sqrt(jnp.where(lane < cols - shift, first, second))
        limit_local.wait()
        own.wait()
    with jax.named_scope("wait_tot"):
        wait_for(tot_got.at[:n_mp - 1], small_recv.at[2])

    with jax.named_scope("scale"):
        row_mean = jnp.sum(tot_got[...], axis=0) / IN + small_eps
        a = gate_slope / row_mean
        b = 0.5 - gate_slope * limits[...]
        for h in range(rows // LANES):
            part = slice(h * LANES, (h + 1) * LANES)
            scale_a[part] = jnp.broadcast_to(a[:, part], (LANES, LANES)).T
            scale_b[part] = jnp.broadcast_to(b[:, part], (LANES, LANES)).T
        wait_for(sq_got.at[:peers], small_send.at[0])
        wait_for(row_got.at[:peers], small_send.at[1])
        wait_for(tot_got.at[:n_mp - 1], small_send.at[2])

    def finish(j):
        span = pl.ds(pl.multiple_of(j * LANES, LANES), LANES)
        wide = got[span].T.astype(jnp.float32)
        scores = jnp.abs(wide) * norms[j]
        kept = jnp.clip(scores * scale_a[...] + scale_b[...], 0.0, 1.0)
        out_ref[:, span] = (wide * kept).astype(jnp.bfloat16)

    mine = sides[3]
    with jax.named_scope("early"):
        for k in range(3):
            wait_for(got.at[place_of(0, depth)], bulk_recv.at[k])

        def early(j):
            t = lax.rem(lax.rem(j, per_group), 4)

            @pl.when(jnp.logical_and(t != mine, lax.rem(t + 1, 4) != mine))
            def _():
                finish(j)

        loop(0, chunks, early)

    def late(i):
        hop = depth // 2 + jnp.where(lax.rem(i, 2) == 0, lax.div(i, 2), -lax.div(i + 1, 2))
        s = lax.rem(z + depth - hop, depth) * 4 + mine

        @pl.when(i < depth - 1)
        def _():
            wait_for(got.at[place_of(s)], bulk_recv.at[3 + i])

        q, u = lax.div(s, 8), lax.rem(s, 8)

        @pl.when(u > 0)
        def _():
            finish(q * per_group + u - 1)

        @pl.when(u < per_group)
        def _():
            finish(q * per_group + u)

    with jax.named_scope("late"):
        loop(0, depth - 1, lambda i: late(jnp.where(i == 0, depth - 1, i - 1)))
    with jax.named_scope("last"):
        late(depth - 2)

    with jax.named_scope("drain"):
        wait_for(got.at[place_of(0, peers)], bulk_send)


def solution(mesh):
    n_dp, n_mp = mesh.shape["dp"], mesh.shape["mp"]

    def per_device(activations, weight, thresholds):
        columns = weight.T
        cols, outs = columns.shape
        rows = outs // n_dp
        width = activations.shape[1]
        steps = 8
        dma = pltpu.SemaphoreType.DMA
        hbm, vmem = pl.BlockSpec(memory_space=pltpu.HBM), pl.BlockSpec(memory_space=pltpu.VMEM)
        return pl.pallas_call(
            functools.partial(kernel, n_dp, n_mp),
            out_shape=pltpu.VMEM((rows, width), jnp.bfloat16),
            in_specs=[hbm, hbm, hbm],
            out_specs=vmem,
            scratch_shapes=[
                pltpu.VMEM(activations.shape, jnp.bfloat16),
                pltpu.VMEM(columns.shape, jnp.bfloat16),
                pltpu.VMEM((n_dp * cols, rows), jnp.bfloat16),
                pltpu.VMEM((n_dp, 1, LANES), jnp.float32),
                pltpu.VMEM((n_dp, 1, LANES), jnp.float32),
                pltpu.VMEM((n_dp, 1, rows + LANES), jnp.float32),
                pltpu.VMEM((n_dp, 1, rows + LANES), jnp.float32),
                pltpu.VMEM((1, rows), jnp.float32),
                pltpu.VMEM((n_mp, 1, rows), jnp.float32),
                pltpu.VMEM((width // LANES, 1, LANES), jnp.float32),
                pltpu.VMEM((1, rows), jnp.float32),
                pltpu.VMEM((rows, LANES), jnp.float32),
                pltpu.VMEM((rows, LANES), jnp.float32),
                dma((steps,)), dma((3,)), dma, dma((n_dp // 4 + 2,)), dma((3,)), dma((3,)),
            ],
            compiler_params=pltpu.CompilerParams(collective_id=0, has_side_effects=True, vmem_limit_bytes=40 * 2**20),
        )(*(pltpu.with_memory_space_constraint(x, pltpu.HBM) for x in (activations, columns, thresholds.reshape(1, rows))))

    placed = (P("dp", "mp"), P(None, ("mp", "dp")), P("dp"))
    return jax.shard_map(per_device, mesh=mesh, in_specs=placed, out_specs=P("dp", "mp"), check_vma=False)
```

time: 99.9 us -> 56.3 us (0.56); the launches traced: 98.6 us -> 56.2 us
  waiting for transfers between devices: 58.4 us -> 0 us
  Pallas kernels: 0 us -> 55 us
  starting transfers between devices: 18.5 us -> 0 us
  blocking collectives: 8.96 us -> 0 us
  other arithmetic: 6.43 us -> 0 us
  local copies, waits for them, and re-layouts: 6.26 us -> 1.23 us
    all_to_all x2 -> x0, waiting for transfers between devices: 58.4 us -> none  [the longest x1 44.2 us: per_device(): lax.all_to_all(weight, 'dp', split_axis=0, concat_axis=1, tiled=True)]
    pallas_call x0 -> x1, Pallas kernels: none -> 55 us  [per_device(): pl.pallas_call(functools.partial(kernel, n_dp, n_mp), out_shape=pltpu.VME...]
    all_to_all x2 -> x0, starting transfers between devices: 18.5 us -> none  [the longest x1 12.7 us: sent_to_all(): return lax.all_to_all(copies, axis, split_axis=0, concat_axis=0, tiled=True)]
    all_to_all x1 -> x0, blocking collectives: 8.96 us -> none  [sent_to_all(): return lax.all_to_all(copies, axis, split_axis=0, concat_axis=0, tiled=True)]
    convert_element_type x1 -> x0, local copies, waits for them, and re-layouts: 3.8 us -> none  [soft_prune(): return (wide * kept_share).astype(jnp.bfloat16)]
    reduce_sum x4 -> x0, other arithmetic: 3.77 us -> none  [the longest x1 2.92 us: per_device(): partial_value = jnp.sum(jnp.square(activations.astype(jnp.float32)), axis=0)]
    convert_element_type x1 -> x0, other arithmetic: 2.65 us -> none  [soft_prune(): return (wide * kept_share).astype(jnp.bfloat16)]
    all_to_all x1 -> x0, local copies, waits for them, and re-layouts: 1.35 us -> none  [per_device(): lax.all_to_all(weight, 'dp', split_axis=0, concat_axis=1, tiled=True)]
  transfers between devices with their start and end apart: 2 -> 0, of which waited for: 2 -> 0; matrix products, arithmetic and copies ran while one was open for 2% -> 0% of each run, Pallas kernels for 0% -> 0%
where the time goes in v1:
time: 56.3 us; the launch traced here: 56.2 us
  Pallas kernels  55 us (98%)
  local copies, waits for them, and re-layouts  1.23 us (2%)
    pallas_call x1, Pallas kernels, per_device(): pl.pallas_call(functools.partial(kernel, n_dp, n_mp), out_shape=pltpu.VME...  55 us
    unnamed x1, local copies, waits for them, and re-layouts  1.23 us

profile of v1, /device:TPU:1, one launch (start us, length us, event | category | flops | bytes accessed | tf_op | source)
XLA Modules:
  0.0 56.2 jit_solution(17866586765136987967)
XLA Ops:
  0.0 55.0 %shard_map.37 = bf16[256,3584]{1,0:T(8,128)(2,1)S(1)} custom-call(bf16[512,3584]{1,0:T(8,128)(2,1)} %act_hbm.1, bf16[112,8192]{1,0:T(8,128)(2,1)} %bitcast.2, f32[1,256]{1,0:T(1,128)} %bitcast.3), custom_call_target="tpu_custom_call" | custom-call | tf_op jit(solution)/shard_map/pallas_call | solution.py:257
  55.0 1.2 %copy.5 = bf16[256,3584]{1,0:T(8,128)(2,1)} copy(bf16[256,3584]{1,0:T(8,128)(2,1)S(1)} %shard_map.37) | data formatting | bytes 3670016

commit v2 on v1

v2 whole, which is shorter than its diff:
```python
import functools

import jax
import jax.numpy as jnp
from jax import lax
from jax.experimental import pallas as pl
from jax.experimental.pallas import tpu as pltpu
from jax.sharding import PartitionSpec as P

IN = 28672
LANES = 128
MESH = pl.DeviceIdType.MESH

gate_slope = 2.0
small_eps = 1e-06


NEAR = [(1, 3), (7, 3), (1, 2), (7, 2), (0, 2), (1, 0), (7, 0), (1, 1), (7, 1), (0, 0), (0, 1)]
FAR_HOPS = [4, 3, 5, 2, 6]
STAGES = [11, 22, 31]


def kernel(
    n_dp, n_mp, act_hbm, wt_hbm, thr_hbm, out_ref,
    act, wt, got, sq_send, sq_got, norm_all, norms, row_send, row_side, row_sum, row_z, tot_send, tot_got,
    limits, scale_a, scale_b,
    act_sem, local_sem, bulk_send, bulk_recv, small_send, small_recv, ring_sem,
):
    d, m = lax.axis_index("dp"), lax.axis_index("mp")
    cols, outs = wt_hbm.shape
    rows = outs // n_dp
    groups = n_dp // 8
    per_group = cols * 8 // LANES
    chunks = groups * per_group
    steps = act_sem.shape[0]
    tokens = act_hbm.shape[0] // steps
    depth = n_dp // 4
    peers = n_dp - 1

    z, high, core = lax.div(d, 4), lax.rem(lax.div(d, 2), 2), lax.rem(d, 2)
    sides = ((1 - high) * 2 + core, (1 - high) * 2 + 1 - core, high * 2 + 1 - core, high * 2 + core)
    mine = sides[3]
    blocks = NEAR + [(hop, side) for side in range(4) for hop in FAR_HOPS]
    assert sorted(blocks) == sorted((hop, side) for hop in range(depth) for side in range(4) if (hop, side) != (0, 3))
    SQUARES, ROW_SIDE, NORM_Z, ROW_Z, NORM_SIDE, TOTAL = range(6)

    def device(hop, side):
        return lax.rem(z + hop, depth) * 4 + sides[side]

    def mp_peer(i):
        return lax.rem(m + i, n_mp)

    def act_copy(i):
        span = pl.ds(pl.multiple_of(i * tokens, tokens), tokens)
        return pltpu.make_async_copy(act_hbm.at[span], act.at[span], act_sem.at[i])

    def block(i):
        return pl.ds(pl.multiple_of(i * rows, rows), rows)

    def place_of(i, n=1):
        return pl.ds(pl.multiple_of(i * cols, 16), n * cols)

    def remote(src, dst, ssem, rsem, to, row=None):
        pltpu.make_async_remote_copy(
            src_ref=src, dst_ref=dst, send_sem=ssem, recv_sem=rsem,
            device_id=(to, m) if row is None else (d, row), device_id_type=MESH,
        ).start()

    def bulk(stage):
        for hop, side in blocks[STAGES[stage - 1] if stage else 0:STAGES[stage]]:
            to = device(hop, side)
            i = 0 if (hop, side) in NEAR else 1 + side if side < 3 else 4 + FAR_HOPS.index(hop)
            remote(wt_hbm.at[:, block(to)], got.at[place_of(d)], bulk_send, bulk_recv.at[i], to)

    def to_plane(n, src, dst):
        for side in range(3):
            remote(src(sides[side]), dst, small_send.at[n], small_recv.at[n], device(0, side))

    def to_column(n, src, dst):
        for hop in (4, 3, 5, 2, 6, 1, 7):
            remote(src(lax.rem(z + hop, depth)), dst, small_send.at[n], small_recv.at[n], device(hop, 3))

    def wait_for(ref, sem):
        pltpu.make_async_copy(ref, ref, sem).wait()

    def loop(lo, hi, body):
        lax.fori_loop(lo, hi, lambda i, c: (body(i), c)[1], 0)

    with jax.named_scope("signal"):
        barrier = pltpu.get_barrier_semaphore()
        for hop in (1, depth - 1, 0):
            for side in range(4):
                if (hop, side) != (0, 3):
                    pl.semaphore_signal(barrier, inc=1, device_id=(device(hop, side), m), device_id_type=MESH)
        for i in range(1, n_mp):
            pl.semaphore_signal(barrier, inc=1, device_id=(d, mp_peer(i)), device_id_type=MESH)

    with jax.named_scope("local"):
        loop(0, steps, lambda i: act_copy(i).start())
        wt_local = pltpu.make_async_copy(wt_hbm, wt, local_sem.at[0])
        wt_local.start()
        own = pltpu.make_async_copy(wt_hbm.at[:, block(d)], got.at[place_of(d)], local_sem.at[1])
        own.start()
        limit_local = pltpu.make_async_copy(thr_hbm, limits, local_sem.at[2])
        limit_local.start()

    def ring_signal(r):
        for hop in (1, depth - 1):
            pl.semaphore_signal(ring_sem.at[r], inc=1, device_id=(device(hop, 3), m), device_id_type=MESH)

    with jax.named_scope("barrier"):
        pl.semaphore_wait(barrier, 11 + n_mp - 1)
    with jax.named_scope("near"):
        ring_signal(0)
        bulk(0)

    with jax.named_scope("squares"):
        def add_squares(i, sums):
            act_copy(i).wait()
            base = pl.multiple_of(i * tokens, tokens)
            out = []
            for j in range(chunks):
                x = act[pl.ds(base, tokens), j * LANES:(j + 1) * LANES].astype(jnp.float32)
                out.append(sums[j] + jnp.sum((x * x).reshape(tokens // 8, 8, LANES), axis=0))
            return tuple(out)

        sums = lax.fori_loop(0, steps, add_squares, tuple(jnp.zeros((8, LANES), jnp.float32) for _ in range(chunks)))
        sums = [jnp.sum(s, axis=0, keepdims=True) for s in sums]
        lane = lax.broadcasted_iota(jnp.int32, (1, LANES), 1)
        for q in range(groups):
            for u in range(8):
                shift = (LANES - cols) * u
                first = sums[per_group * q + max(u - 1, 0)]
                second = sums[per_group * q + min(u, per_group - 1)]
                if u:
                    first = pltpu.roll(first, shift, 1)
                    second = pltpu.roll(second, shift, 1)
                row = jnp.where(lane < shift, first, second)
                sq_send[8 * q + u] = jnp.where(lane < cols, row, 0.0)

    with jax.named_scope("ring0"):
        pl.semaphore_wait(ring_sem.at[0], 2)
        ring_signal(1)
    with jax.named_scope("ring1"):
        pl.semaphore_wait(ring_sem.at[1], 2)
        ring_signal(2)
    with jax.named_scope("ring2"):
        pl.semaphore_wait(ring_sem.at[2], 2)
    with jax.named_scope("issue"):
        for side in range(4):
            for hop in FAR_HOPS + [1, depth - 1, 0]:
                if (hop, side) != (0, 3):
                    to = device(hop, side)
                    remote(sq_send.at[to], sq_got.at[d], small_send.at[SQUARES], small_recv.at[SQUARES], to)
        bulk(1)
        sq_got[d] = sq_send[d]
        wt_local.wait()

    with jax.named_scope("wait_sq"):
        wait_for(sq_got.at[:peers], small_recv.at[SQUARES])

    with jax.named_scope("rowpart"):
        squares = jnp.sum(sq_got[...].reshape(n_dp // 8, 8, LANES), axis=0)
        squares = jnp.sum(squares, axis=0, keepdims=True)
        norm_lane = jnp.sqrt(squares)
        norm = jnp.broadcast_to(norm_lane, (LANES, LANES)).T[:cols]
        norm_all[mine, z] = norm_lane

        def row_part(r):
            for h in range(rows // LANES):
                w = wt[:, pl.ds(pl.multiple_of(r * rows + h * LANES, LANES), LANES)].astype(jnp.float32)
                part = jnp.sum((jnp.abs(w) * norm).reshape(cols // 8, 8, LANES), axis=0)
                row_send[lax.rem(r, 4), lax.div(r, 4), :, h * LANES:(h + 1) * LANES] = jnp.sum(part, axis=0, keepdims=True)

        loop(0, n_dp, row_part)
    with jax.named_scope("send_row"):
        to_plane(ROW_SIDE, lambda s: row_send.at[s], row_side.at[mine])
        to_column(NORM_Z, lambda p: norm_all.at[mine, z], norm_all.at[mine, z])
        row_side[mine] = row_send[mine]
    with jax.named_scope("wait_row"):
        wait_for(row_side.at[:3], small_recv.at[ROW_SIDE])
    with jax.named_scope("send_row2"):
        row_sum[...] = jnp.sum(row_side[...], axis=0)
        row_z[z] = row_sum[z]
        to_column(ROW_Z, lambda p: row_sum.at[p], row_z.at[z])
        bulk(2)
    with jax.named_scope("wait_norm"):
        wait_for(norm_all.at[0, :depth - 1], small_recv.at[NORM_Z])
        to_plane(NORM_SIDE, lambda s: norm_all.at[mine], norm_all.at[mine])
    with jax.named_scope("wait_row2"):
        wait_for(row_z.at[:depth - 1], small_recv.at[ROW_Z])
    with jax.named_scope("tot"):
        tot_send[...] = jnp.sum(row_z[...], axis=0)
        for i in range(1, n_mp):
            remote(tot_send, tot_got.at[m], small_send.at[TOTAL], small_recv.at[TOTAL], d, mp_peer(i))
        tot_got[m] = tot_send[...]
    with jax.named_scope("norms"):
        wait_for(norm_all.at[:3], small_recv.at[NORM_SIDE])
        for q in range(groups):
            for t in range(per_group):
                shift = (LANES - cols) * t
                first = norm_all[t % 4, 2 * q + t // 4]
                second = norm_all[(t + 1) % 4, 2 * q + (t + 1) // 4]
                first = pltpu.roll(first, LANES - shift, 1) if shift else first
                second = pltpu.roll(second, cols - shift, 1)
                norms[per_group * q + t] = jnp.where(lane < cols - shift, first, second)
        limit_local.wait()
        own.wait()
    with jax.named_scope("wait_tot"):
        wait_for(tot_got.at[:n_mp - 1], small_recv.at[TOTAL])

    with jax.named_scope("scale"):
        row_mean = jnp.sum(tot_got[...], axis=0) / IN + small_eps
        a = gate_slope / row_mean
        b = 0.5 - gate_slope * limits[...]
        for h in range(rows // LANES):
            part = slice(h * LANES, (h + 1) * LANES)
            scale_a[part] = jnp.broadcast_to(a[:, part], (LANES, LANES)).T
            scale_b[part] = jnp.broadcast_to(b[:, part], (LANES, LANES)).T
        for n, ref in (
            (SQUARES, sq_got.at[:peers]), (ROW_SIDE, row_side.at[:3]), (NORM_Z, norm_all.at[0, :depth - 1]),
            (ROW_Z, row_z.at[:depth - 1]), (NORM_SIDE, norm_all.at[:3]), (TOTAL, tot_got.at[:n_mp - 1]),
        ):
            wait_for(ref, small_send.at[n])

    def finish(j):
        span = pl.ds(pl.multiple_of(j * LANES, LANES), LANES)
        wide = got[span].T.astype(jnp.float32)
        scores = jnp.abs(wide) * norms[j]
        kept = jnp.clip(scores * scale_a[...] + scale_b[...], 0.0, 1.0)
        out_ref[:, span] = (wide * kept).astype(jnp.bfloat16)

    with jax.named_scope("early_wait"):
        wait_for(got.at[place_of(0, len(NEAR))], bulk_recv.at[0])
        for side in range(3):
            wait_for(got.at[place_of(0, len(FAR_HOPS))], bulk_recv.at[1 + side])

    def is_late(s):
        hop = lax.rem(z + depth - lax.div(s, 4), depth)
        return jnp.logical_and(lax.rem(s, 4) == mine, jnp.logical_and(hop > 1, hop < depth - 1))

    def early(j):
        s = lax.div(j, per_group) * 8 + lax.rem(j, per_group)

        @pl.when(jnp.logical_not(jnp.logical_or(is_late(s), is_late(s + 1))))
        def _():
            finish(j)

    with jax.named_scope("early"):
        loop(0, chunks, early)

    for k, hop in enumerate(FAR_HOPS):
        with jax.named_scope("late%d" % k):
            wait_for(got.at[place_of(0)], bulk_recv.at[4 + k])
            s = lax.rem(z + depth - hop, depth) * 4 + mine
            q, u = lax.div(s, 8), lax.rem(s, 8)
            lo, hi = jnp.where(u > 0, u - 1, 0), jnp.where(u < per_group, u + 1, per_group)
            loop(q * per_group + lo, q * per_group + hi, finish)

    with jax.named_scope("drain"):
        wait_for(got.at[place_of(0, peers)], bulk_send)


def solution(mesh):
    n_dp, n_mp = mesh.shape["dp"], mesh.shape["mp"]

    def per_device(activations, weight, thresholds):
        columns = weight.T
        cols, outs = columns.shape
        rows = outs // n_dp
        width = activations.shape[1]
        steps = 8
        depth = n_dp // 4
        dma = pltpu.SemaphoreType.DMA

        def f32(*shape):
            return pltpu.VMEM(shape, jnp.float32)

        hbm, vmem = pl.BlockSpec(memory_space=pltpu.HBM), pl.BlockSpec(memory_space=pltpu.VMEM)
        return pl.pallas_call(
            functools.partial(kernel, n_dp, n_mp),
            out_shape=pltpu.VMEM((rows, width), jnp.bfloat16),
            in_specs=[hbm, hbm, hbm],
            out_specs=vmem,
            scratch_shapes=[
                pltpu.VMEM(activations.shape, jnp.bfloat16),
                pltpu.VMEM(columns.shape, jnp.bfloat16),
                pltpu.VMEM((n_dp * cols, rows), jnp.bfloat16),
                f32(n_dp, 1, LANES), f32(n_dp, 1, LANES),
                f32(4, depth, 1, LANES), f32(width // LANES, 1, LANES),
                f32(4, depth, 1, rows), f32(4, depth, 1, rows), f32(depth, 1, rows), f32(depth, 1, rows),
                f32(1, rows), f32(n_mp, 1, rows),
                f32(1, rows), f32(rows, LANES), f32(rows, LANES),
                dma((steps,)), dma((3,)), dma, dma((4 + len(FAR_HOPS),)), dma((6,)), dma((6,)), pltpu.SemaphoreType.REGULAR((3,)),
            ],
            compiler_params=pltpu.CompilerParams(collective_id=0, has_side_effects=True, vmem_limit_bytes=40 * 2**20),
        )(*(pltpu.with_memory_space_constraint(x, pltpu.HBM) for x in (activations, columns, thresholds.reshape(1, rows))))

    placed = (P("dp", "mp"), P(None, ("mp", "dp")), P("dp"))
    return jax.shard_map(per_device, mesh=mesh, in_specs=placed, out_specs=P("dp", "mp"), check_vma=False)
```

time: 56.3 us -> 52.9 us (0.940); the launches traced: 56.2 us -> 51.9 us
  Pallas kernels: 55 us -> 50.7 us
    pallas_call x1, Pallas kernels: 55 us -> 50.7 us  [per_device(): pl.pallas_call(functools.partial(kernel, n_dp, n_mp), out_shape=pltpu.VME...]
where the time goes in v2:
time: 52.9 us; the launch traced here: 51.9 us
  Pallas kernels  50.7 us (96%)
  local copies, waits for them, and re-layouts  1.23 us (2%)
    pallas_call x1, Pallas kernels, per_device(): pl.pallas_call(functools.partial(kernel, n_dp, n_mp), out_shape=pltpu.VME...  50.7 us
    unnamed x1, local copies, waits for them, and re-layouts  1.23 us

profile of v2, /device:TPU:1, one launch (start us, length us, event | category | flops | bytes accessed | tf_op | source)
XLA Modules:
  0.0 51.9 jit_solution(10586088844228521840)
XLA Ops:
  0.0 50.7 %shard_map.37 = bf16[256,3584]{1,0:T(8,128)(2,1)S(1)} custom-call(bf16[512,3584]{1,0:T(8,128)(2,1)} %act_hbm.1, bf16[112,8192]{1,0:T(8,128)(2,1)} %bitcast.2, f32[1,256]{1,0:T(1,128)} %bitcast.3), custom_call_target="tpu_custom_call" | custom-call | tf_op jit(solution)/shard_map/pallas_call | solution.py:280
  50.7 1.2 %copy.5 = bf16[256,3584]{1,0:T(8,128)(2,1)} copy(bf16[256,3584]{1,0:T(8,128)(2,1)S(1)} %shard_map.37) | data formatting | bytes 3670016

commit v3 on v2

--- a/solution.py
+++ b/solution.py
@@ -15,16 +15,22 @@
 small_eps = 1e-06
 
 
-NEAR = [(1, 3), (7, 3), (1, 2), (7, 2), (0, 2), (1, 0), (7, 0), (1, 1), (7, 1), (0, 0), (0, 1)]
+SAME = [(1, 3), (7, 3), (1, 2), (7, 2), (0, 2)]
+CROSS = [(1, 0), (7, 0), (1, 1), (7, 1), (0, 0), (0, 1)]
+NEAR = SAME + CROSS
 FAR_HOPS = [4, 3, 5, 2, 6]
-STAGES = [11, 22, 31]
+SWEEPS = [0, 2, 1, 3]
+AHEAD = [(4, 2), (3, 2), (5, 2)]
+ORDER = NEAR + AHEAD + [(hop, side) for side in SWEEPS for hop in FAR_HOPS if (hop, side) not in AHEAD]
+STAGES = [5, 11, 22, 31]
+SPLIT = 4
 
 
 def kernel(
     n_dp, n_mp, act_hbm, wt_hbm, thr_hbm, out_ref,
     act, wt, got, sq_send, sq_got, norm_all, norms, row_send, row_side, row_sum, row_z, tot_send, tot_got,
-    limits, scale_a, scale_b,
-    act_sem, local_sem, bulk_send, bulk_recv, small_send, small_recv, ring_sem,
+    limits, scale_a, scale_b, half,
+    act_sem, local_sem, bulk_send, bulk_recv, small_send, small_recv, ring_sem, cross_sem, row_sem,
 ):
     d, m = lax.axis_index("dp"), lax.axis_index("mp")
     cols, outs = wt_hbm.shape
@@ -40,8 +46,7 @@
     z, high, core = lax.div(d, 4), lax.rem(lax.div(d, 2), 2), lax.rem(d, 2)
     sides = ((1 - high) * 2 + core, (1 - high) * 2 + 1 - core, high * 2 + 1 - core, high * 2 + core)
     mine = sides[3]
-    blocks = NEAR + [(hop, side) for side in range(4) for hop in FAR_HOPS]
-    assert sorted(blocks) == sorted((hop, side) for hop in range(depth) for side in range(4) if (hop, side) != (0, 3))
+    assert sorted(ORDER) == sorted((hop, side) for hop in range(depth) for side in range(4) if (hop, side) != (0, 3))
     SQUARES, ROW_SIDE, NORM_Z, ROW_Z, NORM_SIDE, TOTAL = range(6)
 
     def device(hop, side):
@@ -67,7 +72,7 @@
         ).start()
 
     def bulk(stage):
-        for hop, side in blocks[STAGES[stage - 1] if stage else 0:STAGES[stage]]:
+        for hop, side in ORDER[STAGES[stage - 1] if stage else 0:STAGES[stage]]:
             to = device(hop, side)
             i = 0 if (hop, side) in NEAR else 1 + side if side < 3 else 4 + FAR_HOPS.index(hop)
             remote(wt_hbm.at[:, block(to)], got.at[place_of(d)], bulk_send, bulk_recv.at[i], to)
@@ -86,14 +91,24 @@
     def loop(lo, hi, body):
         lax.fori_loop(lo, hi, lambda i, c: (body(i), c)[1], 0)
 
+    upper, leader = high == 1, m == n_mp - 1
+
+    def signal(sem, to, row=None):
+        pl.semaphore_signal(sem, inc=1, device_id=(to, m) if row is None else (d, row), device_id_type=MESH)
+
     with jax.named_scope("signal"):
         barrier = pltpu.get_barrier_semaphore()
-        for hop in (1, depth - 1, 0):
-            for side in range(4):
-                if (hop, side) != (0, 3):
-                    pl.semaphore_signal(barrier, inc=1, device_id=(device(hop, side), m), device_id_type=MESH)
-        for i in range(1, n_mp):
-            pl.semaphore_signal(barrier, inc=1, device_id=(d, mp_peer(i)), device_id_type=MESH)
+        for hop, side in SAME:
+            signal(barrier, device(hop, side))
+
+        @pl.when(jnp.logical_not(upper))
+        def _():
+            for hop, side in CROSS:
+                signal(barrier, device(hop, side))
+
+        @pl.when(jnp.logical_not(leader))
+        def _():
+            signal(barrier, d, n_mp - 1)
 
     with jax.named_scope("local"):
         loop(0, steps, lambda i: act_copy(i).start())
@@ -106,13 +121,22 @@
 
     def ring_signal(r):
         for hop in (1, depth - 1):
-            pl.semaphore_signal(ring_sem.at[r], inc=1, device_id=(device(hop, 3), m), device_id_type=MESH)
+            signal(ring_sem.at[r], device(hop, 3))
 
     with jax.named_scope("barrier"):
-        pl.semaphore_wait(barrier, 11 + n_mp - 1)
+        pl.semaphore_wait(barrier, len(SAME) + len(CROSS) * upper.astype(jnp.int32) + (n_mp - 1) * leader.astype(jnp.int32))
     with jax.named_scope("near"):
         ring_signal(0)
         bulk(0)
+
+        @pl.when(upper)
+        def _():
+            signal(cross_sem.at[0], device(0, 0))
+
+        @pl.when(leader)
+        def _():
+            for i in range(1, n_mp):
+                signal(row_sem, d, mp_peer(i))
 
     with jax.named_scope("squares"):
         def add_squares(i, sums):
@@ -124,7 +148,20 @@
                 out.append(sums[j] + jnp.sum((x * x).reshape(tokens // 8, 8, LANES), axis=0))
             return tuple(out)
 
-        sums = lax.fori_loop(0, steps, add_squares, tuple(jnp.zeros((8, LANES), jnp.float32) for _ in range(chunks)))
+        sums = lax.fori_loop(0, SPLIT, add_squares, tuple(jnp.zeros((8, LANES), jnp.float32) for _ in range(chunks)))
+        for j in range(chunks):
+            half[j] = sums[j]
+    with jax.named_scope("ring0"):
+        pl.semaphore_wait(ring_sem.at[0], 2)
+        ring_signal(1)
+
+        @pl.when(jnp.logical_not(upper))
+        def _():
+            pl.semaphore_wait(cross_sem.at[0], 1)
+
+        bulk(1)
+    with jax.named_scope("squares2"):
+        sums = lax.fori_loop(SPLIT, steps, add_squares, tuple(half[j] for j in range(chunks)))
         sums = [jnp.sum(s, axis=0, keepdims=True) for s in sums]
         lane = lax.broadcasted_iota(jnp.int32, (1, LANES), 1)
         for q in range(groups):
@@ -138,21 +175,25 @@
                 row = jnp.where(lane < shift, first, second)
                 sq_send[8 * q + u] = jnp.where(lane < cols, row, 0.0)
 
-    with jax.named_scope("ring0"):
-        pl.semaphore_wait(ring_sem.at[0], 2)
-        ring_signal(1)
+    def send_squares(sides_of):
+        for side in sides_of:
+            for hop in FAR_HOPS + [1, depth - 1, 0]:
+                if (hop, side) != (0, 3):
+                    to = device(hop, side)
+                    remote(sq_send.at[to], sq_got.at[d], small_send.at[SQUARES], small_recv.at[SQUARES], to)
+
     with jax.named_scope("ring1"):
         pl.semaphore_wait(ring_sem.at[1], 2)
         ring_signal(2)
     with jax.named_scope("ring2"):
         pl.semaphore_wait(ring_sem.at[2], 2)
+        signal(cross_sem.at[1], device(0, 0))
+        send_squares((2, 3))
+    with jax.named_scope("cross"):
+        pl.semaphore_wait(cross_sem.at[1], 1)
     with jax.named_scope("issue"):
-        for side in range(4):
-            for hop in FAR_HOPS + [1, depth - 1, 0]:
-                if (hop, side) != (0, 3):
-                    to = device(hop, side)
-                    remote(sq_send.at[to], sq_got.at[d], small_send.at[SQUARES], small_recv.at[SQUARES], to)
-        bulk(1)
+        send_squares((0, 1))
+        bulk(2)
         sq_got[d] = sq_send[d]
         wt_local.wait()
 
@@ -183,7 +224,7 @@
         row_sum[...] = jnp.sum(row_side[...], axis=0)
         row_z[z] = row_sum[z]
         to_column(ROW_Z, lambda p: row_sum.at[p], row_z.at[z])
-        bulk(2)
+        bulk(3)
     with jax.named_scope("wait_norm"):
         wait_for(norm_all.at[0, :depth - 1], small_recv.at[NORM_Z])
         to_plane(NORM_SIDE, lambda s: norm_all.at[mine], norm_all.at[mine])
@@ -191,6 +232,11 @@
         wait_for(row_z.at[:depth - 1], small_recv.at[ROW_Z])
     with jax.named_scope("tot"):
         tot_send[...] = jnp.sum(row_z[...], axis=0)
+
+        @pl.when(jnp.logical_not(leader))
+        def _():
+            pl.semaphore_wait(row_sem, 1)
+
         for i in range(1, n_mp):
             remote(tot_send, tot_got.at[m], small_send.at[TOTAL], small_recv.at[TOTAL], d, mp_peer(i))
         tot_got[m] = tot_send[...]
@@ -271,7 +317,7 @@
         width = activations.shape[1]
         steps = 8
         depth = n_dp // 4
-        dma = pltpu.SemaphoreType.DMA
+        dma, regular = pltpu.SemaphoreType.DMA, pltpu.SemaphoreType.REGULAR
 
         def f32(*shape):
             return pltpu.VMEM(shape, jnp.float32)
@@ -290,8 +336,8 @@
                 f32(4, depth, 1, LANES), f32(width // LANES, 1, LANES),
                 f32(4, depth, 1, rows), f32(4, depth, 1, rows), f32(depth, 1, rows), f32(depth, 1, rows),
                 f32(1, rows), f32(n_mp, 1, rows),
-                f32(1, rows), f32(rows, LANES), f32(rows, LANES),
-                dma((steps,)), dma((3,)), dma, dma((4 + len(FAR_HOPS),)), dma((6,)), dma((6,)), pltpu.SemaphoreType.REGULAR((3,)),
+                f32(1, rows), f32(rows, LANES), f32(rows, LANES), f32(width // LANES, 8, LANES),
+                dma((steps,)), dma((3,)), dma, dma((4 + len(FAR_HOPS),)), dma((6,)), dma((6,)), regular((3,)), regular((2,)), regular,
             ],
             compiler_params=pltpu.CompilerParams(collective_id=0, has_side_effects=True, vmem_limit_bytes=40 * 2**20),
         )(*(pltpu.with_memory_space_constraint(x, pltpu.HBM) for x in (activations, columns, thresholds.reshape(1, rows))))

time: 52.9 us -> 52.1 us (0.985); the launches traced: 51.9 us -> 52 us
  no operation moved by 1% of the time
where the time goes in v3:
time: 52.1 us; the launch traced here: 52 us
  Pallas kernels  50.8 us (98%)
  local copies, waits for them, and re-layouts  1.23 us (2%)
    pallas_call x1, Pallas kernels, per_device(): pl.pallas_call(functools.partial(kernel, n_dp, n_mp), out_shape=pltpu.VME...  50.8 us
    unnamed x1, local copies, waits for them, and re-layouts  1.23 us

profile of v3, /device:TPU:1, one launch (start us, length us, event | category | flops | bytes accessed | tf_op | source)
XLA Modules:
  0.0 52.0 jit_solution(3337202429818524514)
XLA Ops:
  0.0 50.8 %shard_map.37 = bf16[256,3584]{1,0:T(8,128)(2,1)S(1)} custom-call(bf16[512,3584]{1,0:T(8,128)(2,1)} %act_hbm.1, bf16[112,8192]{1,0:T(8,128)(2,1)} %bitcast.2, f32[1,256]{1,0:T(1,128)} %bitcast.3), custom_call_target="tpu_custom_call" | custom-call | tf_op jit(solution)/shard_map/pallas_call | solution.py:326
  50.8 1.2 %copy.5 = bf16[256,3584]{1,0:T(8,128)(2,1)} copy(bf16[256,3584]{1,0:T(8,128)(2,1)S(1)} %shard_map.37) | data formatting | bytes 3670016

commit v4 on v3

--- a/solution.py
+++ b/solution.py
@@ -20,10 +20,9 @@
 NEAR = SAME + CROSS
 FAR_HOPS = [4, 3, 5, 2, 6]
 SWEEPS = [0, 2, 1, 3]
-AHEAD = [(4, 2), (3, 2), (5, 2)]
-ORDER = NEAR + AHEAD + [(hop, side) for side in SWEEPS for hop in FAR_HOPS if (hop, side) not in AHEAD]
+ORDER = NEAR + [(hop, side) for side in SWEEPS for hop in FAR_HOPS]
 STAGES = [5, 11, 22, 31]
-SPLIT = 4
+SPLIT = 0
 
 
 def kernel(
@@ -75,7 +74,7 @@
         for hop, side in ORDER[STAGES[stage - 1] if stage else 0:STAGES[stage]]:
             to = device(hop, side)
             i = 0 if (hop, side) in NEAR else 1 + side if side < 3 else 4 + FAR_HOPS.index(hop)
-            remote(wt_hbm.at[:, block(to)], got.at[place_of(d)], bulk_send, bulk_recv.at[i], to)
+            remote((wt_hbm if stage < 2 else wt).at[:, block(to)], got.at[place_of(d)], bulk_send, bulk_recv.at[i], to)
 
     def to_plane(n, src, dst):
         for side in range(3):
@@ -193,9 +192,9 @@
         pl.semaphore_wait(cross_sem.at[1], 1)
     with jax.named_scope("issue"):
         send_squares((0, 1))
+        wt_local.wait()
         bulk(2)
         sq_got[d] = sq_send[d]
-        wt_local.wait()
 
     with jax.named_scope("wait_sq"):
         wait_for(sq_got.at[:peers], small_recv.at[SQUARES])

time: 52.1 us -> 51.4 us (0.987)
  Pallas kernels: 50.8 us -> 50.1 us
    pallas_call x1, Pallas kernels: 50.8 us -> 50.1 us  [per_device(): pl.pallas_call(functools.partial(kernel, n_dp, n_mp), out_shape=pltpu.VME...]
where the time goes in v4:
time: 51.4 us; the launch traced here: 51.3 us
  Pallas kernels  50.1 us (97%)
  local copies, waits for them, and re-layouts  1.23 us (2%)
    pallas_call x1, Pallas kernels, per_device(): pl.pallas_call(functools.partial(kernel, n_dp, n_mp), out_shape=pltpu.VME...  50.1 us
    unnamed x1, local copies, waits for them, and re-layouts  1.23 us

profile of v4, /device:TPU:1, one launch (start us, length us, event | category | flops | bytes accessed | tf_op | source)
XLA Modules:
  0.0 51.3 jit_solution(13393498602748681848)
XLA Ops:
  0.0 50.1 %shard_map.37 = bf16[256,3584]{1,0:T(8,128)(2,1)S(1)} custom-call(bf16[512,3584]{1,0:T(8,128)(2,1)} %act_hbm.1, bf16[112,8192]{1,0:T(8,128)(2,1)} %bitcast.2, f32[1,256]{1,0:T(1,128)} %bitcast.3), custom_call_target="tpu_custom_call" | custom-call | tf_op jit(solution)/shard_map/pallas_call | solution.py:325
  50.1 1.2 %copy.5 = bf16[256,3584]{1,0:T(8,128)(2,1)} copy(bf16[256,3584]{1,0:T(8,128)(2,1)S(1)} %shard_map.37) | data formatting | bytes 3670016

commit v5 on v4

--- a/solution.py
+++ b/solution.py
@@ -19,7 +19,7 @@
 CROSS = [(1, 0), (7, 0), (1, 1), (7, 1), (0, 0), (0, 1)]
 NEAR = SAME + CROSS
 FAR_HOPS = [4, 3, 5, 2, 6]
-SWEEPS = [0, 2, 1, 3]
+SWEEPS = [2, 0, 1, 3]
 ORDER = NEAR + [(hop, side) for side in SWEEPS for hop in FAR_HOPS]
 STAGES = [5, 11, 22, 31]
 SPLIT = 0

time: 51.4 us -> 51.3 us (level)
  no operation moved by 1% of the time
where the time goes in v5:
time: 51.3 us; the launch traced here: 51.2 us
  Pallas kernels  50 us (97%)
  local copies, waits for them, and re-layouts  1.23 us (2%)
    pallas_call x1, Pallas kernels, per_device(): pl.pallas_call(functools.partial(kernel, n_dp, n_mp), out_shape=pltpu.VME...  50 us
    unnamed x1, local copies, waits for them, and re-layouts  1.23 us

profile of v5, /device:TPU:1, one launch (start us, length us, event | category | flops | bytes accessed | tf_op | source)
XLA Modules:
  0.0 51.2 jit_solution(14363736289448887504)
XLA Ops:
  0.0 50.0 %shard_map.37 = bf16[256,3584]{1,0:T(8,128)(2,1)S(1)} custom-call(bf16[512,3584]{1,0:T(8,128)(2,1)} %act_hbm.1, bf16[112,8192]{1,0:T(8,128)(2,1)} %bitcast.2, f32[1,256]{1,0:T(1,128)} %bitcast.3), custom_call_target="tpu_custom_call" | custom-call | tf_op jit(solution)/shard_map/pallas_call | solution.py:325
  50.0 1.2 %copy.5 = bf16[256,3584]{1,0:T(8,128)(2,1)} copy(bf16[256,3584]{1,0:T(8,128)(2,1)S(1)} %shard_map.37) | data formatting | bytes 3670016
